TPU v7x, 32 devices: a whole 2x2x4 slice. The times are simulated.
32 devices in a mesh: grp: 4 (over x, core), dev: 8 (over z, y).
Axes of the slice: x: 2, y: 2, z: 4, core: 2. Of those that a mesh axis runs over, the one named last changes fastest.
Arguments:
- node_features: float32 [16384, 768], P(('grp', 'dev')), may hold values from -6 to 6
- tiles: bfloat16 [896, 128, 128], P(('grp', 'dev')), may hold values from -0.1875 to 0.1875
- tile_list: int32 [896, 2], replicated, may hold values from 0 to 127, as said below
- weight: float32 [768, 768], replicated, may hold values from -0.21875 to 0.21875
- texts: float32 [1024, 768], P(('grp', 'dev')), may hold values from -6 to 6
- selected: int32 [1024], P(('grp', 'dev')), may hold values from 0 to 16383, as said below
- pairing: int32 [1024], P(('grp', 'dev')), may hold values from 0 to 1023, each once
Outputs:
- contrast_loss: float32 [], replicated
- grad_nodes: float32 [16384, 768], P(('grp', 'dev'))
- grad_weight: float32 [768, 768], replicated
- grad_texts: float32 [1024, 768], P(('grp', 'dev'))
Inputs may be any that keep to these rules, and one draw needn't show every extreme that they name: `tile_list`: device number p = grp index * (devices along dev) + dev index holds node blocks p * 4 to (p + 1) * 4 - 1 and tiles p * 28 to (p + 1) * 28 - 1. A tile's row block lies on the device that holds the tile; its column block lies on that device, on another device of the same grp index, or on the device of the same dev index in another grp. At most 2 tiles of one device have column blocks on any one other device; in every draw each device has one other device of its grp index and one of its dev index at that most. `selected`: distinct ids; the ids listed on a device are nodes of that device.
All inputs are finite; a program needn't handle non-finite values.
Results may differ from a plain program's by a relative error of at most 0.0004.
The roundings to bfloat16 on the way count: a program that leaves them out, or rounds other values in their place, can miss the bound.
Values may be sent and summed in bfloat16 or wider, within the bound.
No kernel may reach another device: no remote copies, remote signals or barrier semaphores. Data moves between devices by JAX's collectives and lax.ppermute only.
A program may use at most 128 MiB of HBM per device.

v0:
```python
import jax
import jax.numpy as jnp
from jax import lax
from jax.sharding import PartitionSpec as P

CAP = 2
SCALE = 1.0 / 0.07
EPS = 1e-06
PRECISE = lax.Precision.HIGHEST
ROOT_HALF = 0.7071067811865476
INV_ROOT_TWO_PI = 0.3989422804014327


def gelu_value(value):
    return 0.5 * value * (1.0 + lax.erf(value * ROOT_HALF))


def gelu_slope(value):
    return (
        0.5 * (1.0 + lax.erf(value * ROOT_HALF))
        + value * jnp.exp(-0.5 * value * value) * INV_ROOT_TWO_PI
    )


def slot_plan(peer_lists, peer_ids, device, blocks_dev, capacity):
    col_owner = peer_lists[:, :, 1] // blocks_dev
    wanted = (col_owner == device) & (peer_ids[:, None] != device)
    slot_order = jnp.cumsum(wanted.astype(jnp.int32), axis=1) - 1
    local_block = peer_lists[:, :, 1] - device * blocks_dev
    slot_hits = wanted[:, :, None] & (
        slot_order[:, :, None] == jnp.arange(capacity, dtype=jnp.int32)[None, None, :]
    )
    block_index = jnp.sum(jnp.where(slot_hits, local_block[:, :, None], 0), axis=1)
    slot_valid = jnp.any(slot_hits, axis=1)
    return (block_index.reshape(-1), slot_valid.reshape(-1))


def slot_pick(slot_of_tile, keep, slots_all):
    return (slot_of_tile[None, :] == jnp.arange(slots_all, dtype=jnp.int32)[:, None]) & keep[
        None, :
    ]


def land_blocks(total, block_index, valid, incoming):
    return total.at[block_index].add(jnp.where(valid[:, None, None], incoming, 0.0))


def shards(node_features, tiles, tile_list, weight, texts, selected, pairing):
    groups = lax.axis_size("grp")
    members = lax.axis_size("dev")
    grp_index = lax.axis_index("grp")
    dev_index = lax.axis_index("dev")
    device = grp_index * members + dev_index
    block_rows = tiles.shape[1]
    feat_width = node_features.shape[1]
    blocks_dev = node_features.shape[0] // block_rows
    tile_dev = tiles.shape[0]
    sel_dev = selected.shape[0]
    capacity = CAP
    total_sel = sel_dev * groups * members
    rounded = node_features.astype(jnp.bfloat16).reshape(blocks_dev, block_rows, feat_width)
    my_list = lax.dynamic_slice_in_dim(tile_list, device * tile_dev, tile_dev, 0)
    row_block = my_list[:, 0] - device * blocks_dev
    col_owner = my_list[:, 1] // blocks_dev
    col_block = my_list[:, 1] - col_owner * blocks_dev
    owner_grp = col_owner // members
    owner_dev = col_owner % members
    is_local = col_owner == device
    is_near = (owner_grp == grp_index) & jnp.logical_not(is_local)
    is_far = (owner_dev == dev_index) & (owner_grp != grp_index)
    positions = jnp.arange(tile_dev, dtype=jnp.int32)
    earlier = (col_owner[:, None] == col_owner[None, :]) & (positions[None, :] < positions[:, None])
    slot_rank = jnp.sum(earlier.astype(jnp.int32), axis=1)
    near_slot = owner_dev * capacity + slot_rank
    far_slot = owner_grp * capacity + slot_rank
    group_lists = lax.dynamic_slice_in_dim(
        tile_list, grp_index * members * tile_dev, members * tile_dev, 0
    ).reshape(members, tile_dev, 2)
    near_peers = grp_index * members + jnp.arange(members, dtype=jnp.int32)
    near_index, near_valid = slot_plan(group_lists, near_peers, device, blocks_dev, capacity)
    far_lists = lax.dynamic_index_in_dim(
        tile_list.reshape(groups, members, tile_dev, 2), dev_index, 1, False
    )
    far_peers = jnp.arange(groups, dtype=jnp.int32) * members + dev_index
    far_index, far_valid = slot_plan(far_lists, far_peers, device, blocks_dev, capacity)
    zero_half = jnp.zeros((), jnp.bfloat16)
    sel_local = selected - device * blocks_dev * block_rows
    sel_block = sel_local // block_rows
    sel_offset = sel_local % block_rows
    picked = jnp.take(tiles, sel_offset, axis=1)
    tile_rows = jnp.where((row_block[:, None] == sel_block[None, :])[:, :, None], picked, zero_half)
    near_pick = slot_pick(near_slot, is_near, members * capacity)
    far_pick = slot_pick(far_slot, is_far, groups * capacity)
    near_rows = jnp.einsum(
        "st,tkc->skc", near_pick.astype(jnp.bfloat16), tile_rows, preferred_element_type=jnp.float32
    ).astype(jnp.bfloat16)
    far_rows = jnp.einsum(
        "st,tkc->skc", far_pick.astype(jnp.bfloat16), tile_rows, preferred_element_type=jnp.float32
    ).astype(jnp.bfloat16)
    local_tile_rows = jnp.where(is_local[:, None, None], tile_rows, zero_half)
    near_send = jnp.where(
        near_valid[:, None, None], jnp.take(rounded, near_index, axis=0), zero_half
    )
    near_blocks = lax.all_to_all(
        near_send.reshape(members, capacity, block_rows, feat_width),
        "dev",
        split_axis=0,
        concat_axis=0,
        tiled=True,
    )
    far_send = jnp.where(far_valid[:, None, None], jnp.take(rounded, far_index, axis=0), zero_half)
    far_blocks = lax.all_to_all(
        far_send.reshape(groups, capacity, block_rows, feat_width),
        "grp",
        split_axis=0,
        concat_axis=0,
        tiled=True,
    )
    source_table = jnp.concatenate(
        [
            rounded,
            near_blocks.reshape(-1, block_rows, feat_width),
            far_blocks.reshape(-1, block_rows, feat_width),
        ],
        axis=0,
    )
    source_index = jnp.where(
        is_local,
        col_block,
        jnp.where(is_near, blocks_dev + near_slot, blocks_dev + members * capacity + far_slot),
    )
    sources = jnp.take(source_table, source_index, axis=0)
    messages = jnp.einsum("tkc,tcd->kd", tile_rows, sources, preferred_element_type=jnp.float32)
    chosen = node_features[sel_local] + messages
    before = jnp.dot(chosen, weight, precision=PRECISE)
    hidden = gelu_value(before)
    node_norm = jnp.sqrt(jnp.sum(hidden * hidden, axis=1, keepdims=True) + EPS)
    unit_nodes = hidden / node_norm
    text_norm = jnp.sqrt(jnp.sum(texts * texts, axis=1, keepdims=True) + EPS)
    unit_texts = texts / text_norm
    node_rows, pair_rows = (
        lax.all_gather(unit_nodes, "dev", axis=0, tiled=True),
        lax.all_gather(pairing, "dev", axis=0, tiled=True),
    )
    text_cols = lax.all_gather(unit_texts, "grp", axis=0, tiled=True)
    scores = SCALE * lax.dot_general(
        node_rows, text_cols, (((1,), (1,)), ((), ())), precision=PRECISE
    )
    exp_scores = jnp.exp(scores)
    row_total = lax.psum(jnp.sum(exp_scores, axis=1), "dev")
    col_total = lax.psum(jnp.sum(exp_scores, axis=0), "grp")
    col_global = (
        (jnp.arange(groups, dtype=jnp.int32)[:, None] * members + dev_index) * sel_dev
        + jnp.arange(sel_dev, dtype=jnp.int32)[None, :]
    ).reshape(-1)
    target = pair_rows[:, None] == col_global[None, :]
    score_grads = 0.5 * (
        exp_scores / row_total[:, None] + exp_scores / col_total[None, :]
    ) - target.astype(jnp.float32)
    node_part = SCALE * jnp.dot(score_grads, text_cols, precision=PRECISE)
    node_dir = lax.psum_scatter(node_part, "dev", scatter_dimension=0, tiled=True)
    text_part = SCALE * lax.dot_general(
        score_grads, node_rows, (((0,), (0,)), ((), ())), precision=PRECISE
    )
    text_dir = lax.psum_scatter(text_part, "grp", scatter_dimension=0, tiled=True)
    own_rows = lax.dynamic_slice_in_dim(row_total, dev_index * sel_dev, sel_dev, 0)
    own_cols = lax.dynamic_slice_in_dim(col_total, grp_index * sel_dev, sel_dev, 0)
    positive = jnp.sum(jnp.where(target, scores, 0.0))
    lse_sum, pos_sum = lax.psum(
        (jnp.sum(jnp.log(own_rows)) + jnp.sum(jnp.log(own_cols)), positive), ("grp", "dev")
    )
    contrast_loss = lse_sum / (2.0 * total_sel) - pos_sum / total_sel
    node_back = (
        node_dir - unit_nodes * jnp.sum(unit_nodes * node_dir, axis=1, keepdims=True)
    ) / node_norm
    grad_texts = (
        text_dir - unit_texts * jnp.sum(unit_texts * text_dir, axis=1, keepdims=True)
    ) / text_norm
    pre_grad = node_back * gelu_slope(before)
    weight_term = lax.dot_general(chosen, pre_grad, (((0,), (0,)), ((), ())), precision=PRECISE)
    grad_weight = lax.psum(weight_term, ("grp", "dev"))
    row_grads = lax.dot_general(pre_grad, weight, (((1,), (1,)), ((), ())), precision=PRECISE)
    rounded_grads = row_grads.astype(jnp.bfloat16)
    empty_blocks = jnp.zeros((blocks_dev, block_rows, feat_width), jnp.float32)
    local_spread = jnp.einsum(
        "tkc,kd->tcd", local_tile_rows, rounded_grads, preferred_element_type=jnp.float32
    )
    grad_blocks = empty_blocks.at[col_block].add(local_spread)
    near_rows_in = lax.all_to_all(
        near_rows.reshape(members, capacity, sel_dev, block_rows),
        "dev",
        split_axis=0,
        concat_axis=0,
        tiled=True,
    )
    near_grads_in = lax.all_gather(rounded_grads, "dev", axis=0, tiled=True).reshape(
        members, sel_dev, feat_width
    )
    near_spread = jnp.einsum(
        "pqkc,pkd->pqcd", near_rows_in, near_grads_in, preferred_element_type=jnp.float32
    )
    grad_blocks = land_blocks(
        grad_blocks, near_index, near_valid, near_spread.reshape(-1, block_rows, feat_width)
    )
    far_rows_in = lax.all_to_all(
        far_rows.reshape(groups, capacity, sel_dev, block_rows),
        "grp",
        split_axis=0,
        concat_axis=0,
        tiled=True,
    )
    far_grads_in = lax.all_gather(rounded_grads, "grp", axis=0, tiled=True).reshape(
        groups, sel_dev, feat_width
    )
    far_spread = jnp.einsum(
        "pqkc,pkd->pqcd", far_rows_in, far_grads_in, preferred_element_type=jnp.float32
    )
    grad_blocks = land_blocks(
        grad_blocks, far_index, far_valid, far_spread.reshape(-1, block_rows, feat_width)
    )
    grad_nodes = grad_blocks.reshape(-1, feat_width).at[sel_local].add(row_grads)
    return (contrast_loss, grad_nodes, grad_weight, grad_texts)


def solution(mesh):
    return jax.shard_map(
        shards,
        mesh=mesh,
        in_specs=(
            P(("grp", "dev"), None),
            P(("grp", "dev"), None, None),
            P(),
            P(),
            P(("grp", "dev"), None),
            P(("grp", "dev")),
            P(("grp", "dev")),
        ),
        out_specs=(P(), P(("grp", "dev"), None), P(), P(("grp", "dev"), None)),
        check_vma=False,
    )
```

profile of v0, /device:TPU:0, one launch (start us, length us, event | category | flops | bytes accessed | tf_op | source)
XLA Modules:
  0.0 443.1 jit_solution(16403538620831499144)
XLA Ops:
  7.2 0.9 reshape.393
  8.3 0.2 reduce_window_sum.29
  8.5 0.1 select_reduce_fusion.1
  8.7 0.2 fusion.39
  8.9 1.5 convert_element_type.25
  10.7 1.8 gather_fusion.3
  12.5 2.8 select_select_fusion.1
  15.3 4.4 all-to-all-start.1
  19.7 0.8 constant_dynamic-slice_fusion.1
  20.6 0.2 reduce_window_sum.27
  20.8 0.2 select_reduce_fusion
  21.1 2.5 gather_fusion.2
  23.7 0.1 fusion.26
  23.9 4.0 select_select_fusion
  27.9 12.5 %all-to-all-done.1 = bf16[4,2,128,768]{3,2,1,0:T(8,128)(2,1)} async-done(((bf16[4,2,128,768]{3,2,1,0:T(8,128)(2,1)}), bf16[4,2,128,768]{3,2,1,0:T(8,128)(2,1)}, u32[]{:S(2)}, u32[]{:S(2)}) %all-to-all-start.1) | async-done | bytes 1572896 | tf_op jit(solution)/shard_map/all_to_all | solution.py:112
  40.4 6.6 %all-to-all-start = ((bf16[8,2,128,768]{3,2,1,0:T(8,128)(2,1)}), bf16[8,2,128,768]{3,2,1,0:T(8,128)(2,1)}, u32[]{:S(2)}, u32[]{:S(2)}) async-start(bf16[8,2,128,768]{3,2,1,0:T(8,128)(2,1)} %select_select_fusion), calls=%async_computation | async-start | bytes 6291456 | tf_op jit(solution)/shard_map/all_to_all | solution.py:104
  47.3 2.1 gather_fusion
  49.4 0.6 dynamic-slice
  50.7 2.8 gather_fusion.1
  53.5 0.2 dynamic-update-slice
  53.7 64.1 %all-reduce = s32[256]{0:T(256)S(1)} all-reduce(s32[256]{0:T(256)S(1)} %dynamic-update-slice), channel_id=1, replica_groups=mesh['grp'=4,'dev'=8] {'dev'}, use_global_device_ids=true, to_apply=%add | all-reduce | flops 256 | bytes 2048
  117.7 0.8 constant_dynamic-slice_fusion.2
  118.5 0.2 convert_reduce_fusion
  119.0 6.6 %all_gather.16 = f32[128,768]{1,0:T(8,128)} all-gather(f32[32,768]{1,0:T(8,128)S(1)} %broadcast_divide_fusion), channel_id=1, replica_groups=mesh['grp'=4,'dev'=8] {'grp'}, dimensions={0}, use_global_device_ids=true | all-gather | bytes 491520 | tf_op jit(solution)/shard_map/all_gather | solution.py:145
  125.6 1.1 bitcast_select_fusion.2
  126.8 5.8 %pad_maximum_fusion = bf16[28,128,768]{2,1,0:T(8,128)(2,1)} fusion(bf16[8,128,768]{2,1,0:T(8,128)(2,1)} %bitcast.17, bf16[16,128,768]{2,1,0:T(8,128)(2,1)} %bitcast.11, bf16[4,128,768]{2,1,0:T(8,128)(2,1)S(1)} %bitcast.101), kind=kLoop, calls=%fused_computation.10 | loop fusion | flops 5505024 | bytes 11010048 | tf_op jit(solution)/shard_map/concatenate | solution.py:119
  132.6 6.0 %gather_fusion.4 = bf16[28,128,768]{2,1,0:T(8,128)(2,1)} fusion(bf16[28,128,768]{2,1,0:T(8,128)(2,1)} %pad_maximum_fusion, s32[1024]{0:T(1024)S(1)} %pad_clamp_fusion), kind=kCustom, calls=%fused_computation.4 | custom fusion | bytes 11010160 | tf_op jit(solution)/shard_map/jit(_take)/gather | solution.py:132
  138.6 3.6 fusion.7
  142.2 1.5 multiply_reduce_fusion.3
  143.9 32.1 %all_gather.15 = f32[256,768]{1,0:T(8,128)S(1)} all-gather(f32[32,768]{1,0:T(8,128)S(1)} %broadcast_divide_fusion.1), channel_id=1, replica_groups=mesh['grp'=4,'dev'=8] {'dev'}, dimensions={0}, use_global_device_ids=true | all-gather | bytes 884736 | tf_op jit(solution)/shard_map/all_gather | solution.py:142
  176.0 2.0 fusion.15
  178.0 19.6 %psum.35 = f32[256]{0:T(256)S(1)} all-reduce(f32[256]{0:T(256)S(1)} %get-tuple-element.6), channel_id=1, replica_groups=mesh['grp'=4,'dev'=8] {'dev'}, use_global_device_ids=true, to_apply=%region_10.11 | all-reduce | flops 256 | bytes 2048 | tf_op jit(solution)/shard_map/psum | solution.py:150
  197.6 5.6 %psum.36 = f32[128]{0:T(128)S(1)} all-reduce(f32[128]{0:T(128)S(1)} %get-tuple-element.5), channel_id=1, replica_groups=mesh['grp'=4,'dev'=8] {'grp'}, use_global_device_ids=true, to_apply=%region_13.14 | all-reduce | flops 128 | bytes 1024 | tf_op jit(solution)/shard_map/psum | solution.py:151
  203.3 2.3 convolution_multiply_fusion.1
  205.7 2.8 convolution_multiply_fusion
  208.5 0.2 convolution_convert_fusion
  208.7 0.7 copy.27
  209.4 3.4 all-to-all-start.2
  213.0 0.2 convolution_convert_fusion.1
  213.2 0.6 copy.30
  213.8 0.7 log_reduce_fusion.1
  214.5 0.7 log_reduce_fusion
  216.5 40.7 %all-reduce.1 = (f32[]{:T(128)}, f32[]{:T(128)}) all-reduce(f32[]{:T(128)S(6)} %add.310, f32[]{:T(128)} %get-tuple-element.4), channel_id=1, replica_groups=mesh['grp'=4,'dev'=8] {'grp','dev'}, use_global_device_ids=true, to_apply=%region_15.16 | all-reduce | flops 2 | bytes 16 | tf_op jit(solution)/shard_map/psum | solution.py:169
  258.5 1.1 multiply_reduce_fusion
  259.6 1.6 subtract_divide_fusion
  261.2 29.5 %reduce-scatter.3.cloned.1.call-done = f32[32,768]{1,0:T(8,128)} async-done(((f32[256,768]{1,0:T(8,128)}), f32[32,768]{1,0:T(8,128)}) %reduce-scatter.3.cloned.1.call-update) | async-done | bytes 98320 | tf_op jit(solution)/shard_map/reduce_scatter | solution.py:161
  290.7 1.2 multiply_reduce_fusion.1
  291.9 4.4 fusion.57
  296.3 2.3 fusion.63
  298.5 6.1 %fusion.12 = f32[28,128,768]{2,1,0:T(8,128)} fusion(bf16[28,32,128]{2,1,0:T(8,128)(2,1)S(1)} %bitcast_select_fusion.2, pred[28]{0:T(512)(128)(4,1)S(1)} %get-tuple-element.14, bf16[32,768]{1,0:T(8,128)(2,1)S(1)} %get-tuple-element.34), kind=kOutput, calls=%fused_computation.28 | convolution fusion | flops 176275456 | bytes 11288604 | tf_op jit(solution)/shard_map/tkc,kd->tcd/dot_general | solution.py:185
  304.6 1.3 broadcast_in_dim.214
  305.9 25.5 %scatter_fusion = f32[4,128,768]{2,1,0:T(8,128)} fusion(f32[4,128,768]{2,1,0:T(8,128)} %broadcast_in_dim.214, s32[28]{0:T(128)S(1)} %get-tuple-element.15, f32[28,128,768]{2,1,0:T(8,128)} %fusion.12), kind=kCustom, calls=%fused_computation.5 | custom fusion | flops 2752512 | bytes 33030256 | tf_op jit(solution)/shard_map/scatter-add | solution.py:188
  331.4 31.2 %all_gather.18 = bf16[256,768]{1,0:T(8,128)(2,1)S(1)} all-gather(bf16[32,768]{1,0:T(8,128)(2,1)S(1)} %get-tuple-element.34), channel_id=1, replica_groups=mesh['grp'=4,'dev'=8] {'dev'}, dimensions={0}, use_global_device_ids=true | all-gather | bytes 442368 | tf_op jit(solution)/shard_map/all_gather | solution.py:196
  362.5 3.3 all-to-all-start.3
  365.8 1.0 fusion.64
  366.8 3.4 bitcast_select_fusion
  370.2 14.5 %scatter_fusion.1 = f32[4,128,768]{2,1,0:T(8,128)} fusion(f32[4,128,768]{2,1,0:T(8,128)} %scatter_fusion, s32[16]{0:T(128)S(1)} %fusion.47, f32[16,128,768]{2,1,0:T(8,128)} %bitcast_select_fusion), kind=kCustom, calls=%fused_computation.6 | custom fusion | flops 1572864 | bytes 18874432 | tf_op jit(solution)/shard_map/scatter-add | solution.py:45
  384.8 5.8 %all_gather.19 = bf16[128,768]{1,0:T(8,128)(2,1)S(1)} all-gather(bf16[32,768]{1,0:T(8,128)(2,1)S(1)} %get-tuple-element.34), channel_id=1, replica_groups=mesh['grp'=4,'dev'=8] {'grp'}, dimensions={0}, use_global_device_ids=true | all-gather | bytes 245760 | tf_op jit(solution)/shard_map/all_gather | solution.py:212
  390.6 0.6 fusion.65
  391.2 2.0 bitcast_select_fusion.1
  393.2 7.4 %scatter_fusion.2 = f32[4,128,768]{2,1,0:T(8,128)} fusion(f32[4,128,768]{2,1,0:T(8,128)} %scatter_fusion.1, s32[8]{0:T(128)S(1)} %fusion.48, f32[8,128,768]{2,1,0:T(8,128)} %bitcast_select_fusion.1), kind=kCustom, calls=%fused_computation.7 | custom fusion | flops 786432 | bytes 9437216 | tf_op jit(solution)/shard_map/scatter-add | solution.py:45
  400.7 3.4 scatter_fusion.3
  404.1 28.1 %all-reduce.4.cloned.1.call-done = f32[768,768]{1,0:T(8,128)} async-done(((f32[768,768]{1,0:T(8,128)}), f32[768,768]{1,0:T(8,128)}) %all-reduce.4.cloned.1.call-update) | async-done | bytes 2359312 | tf_op jit(solution)/shard_map/psum | solution.py:181
  432.2 3.2 copy.43
  (78 shorter events, 2.2 us)
Async XLA Ops:
  7.2 135.0 %copy-start = (f32[768,768]{1,0:T(8,128)S(1)}, f32[768,768]{1,0:T(8,128)}, u32[]{:S(2)}) copy-start(f32[768,768]{1,0:T(8,128)} %param.10) | copy-start | bytes 7077892
  15.3 25.1 %all-to-all-start.1 = ((bf16[4,2,128,768]{3,2,1,0:T(8,128)(2,1)}), bf16[4,2,128,768]{3,2,1,0:T(8,128)(2,1)}, u32[]{:S(2)}, u32[]{:S(2)}) async-start(bf16[4,2,128,768]{3,2,1,0:T(8,128)(2,1)} %select_select_fusion.1), calls=%async_computation.1 | async-start | bytes 3145728 | tf_op jit(solution)/shard_map/all_to_all | solution.py:112
  27.9 19.4 %copy-start.8 = (s32[32]{0:T(128)S(1)}, s32[32]{0:T(128)}, u32[]{:S(2)}) copy-start(s32[32]{0:T(128)} %param.12) | copy-start | bytes 388
  27.9 21.5 %copy-start.10 = (u32[32]{0:T(128)S(1)}, u32[32]{0:T(128)}, u32[]{:S(2)}) copy-start(u32[32]{0:T(128)} %constant.215) | copy-start | bytes 388
  27.9 25.5 %copy-start.9 = (s32[32]{0:T(128)S(1)}, s32[32]{0:T(128)}, u32[]{:S(2)}) copy-start(s32[32]{0:T(128)} %param.13) | copy-start | bytes 388
  27.9 90.8 %copy-start.3 = (f32[32,768]{1,0:T(8,128)S(1)}, f32[32,768]{1,0:T(8,128)}, u32[]{:S(2)}) copy-start(f32[32,768]{1,0:T(8,128)} %param.11) | copy-start | bytes 294916
  40.4 86.4 %all-to-all-start = ((bf16[8,2,128,768]{3,2,1,0:T(8,128)(2,1)}), bf16[8,2,128,768]{3,2,1,0:T(8,128)(2,1)}, u32[]{:S(2)}, u32[]{:S(2)}) async-start(bf16[8,2,128,768]{3,2,1,0:T(8,128)(2,1)} %select_select_fusion), calls=%async_computation | async-start | bytes 6291456 | tf_op jit(solution)/shard_map/all_to_all | solution.py:104
  47.1 211.4 %reduce-scatter.5.cloned.1.call-start = ((), (), s32[]{:S(2)}) async-start(), calls=%async_computation.8 | async-start | bytes 491520 | tf_op jit(solution)/shard_map/reduce_scatter | solution.py:165
  142.2 35.8 %copy-start.6 = (f32[32,768]{1,0:T(8,128)}, f32[32,768]{1,0:T(8,128)S(1)}, u32[]{:S(2)}) copy-start(f32[32,768]{1,0:T(8,128)S(1)} %fusion.7) | copy-start | bytes 294916
  142.2 33.8 %copy-start.2 = (f32[128,768]{1,0:T(8,128)S(1)}, f32[128,768]{1,0:T(8,128)}, u32[]{:S(2)}) copy-start(f32[128,768]{1,0:T(8,128)} %all_gather.16) | copy-start | bytes 1179652
  205.6 52.9 %copy-start.4 = (f32[32,768]{1,0:T(8,128)S(1)}, f32[32,768]{1,0:T(8,128)}, u32[]{:S(2)}) copy-start(f32[32,768]{1,0:T(8,128)} %param.11) | copy-start | bytes 294916
  205.6 86.2 %copy-start.7 = (f32[32,768]{1,0:T(8,128)S(1)}, f32[32,768]{1,0:T(8,128)}, u32[]{:S(2)}) copy-start(f32[32,768]{1,0:T(8,128)} %copy-done.6) | copy-start | bytes 294916
  205.6 85.1 %reduce-scatter.3.cloned.1.call-start = ((), (), s32[]{:S(2)}) async-start(), calls=%async_computation.6 | async-start | bytes 884736 | tf_op jit(solution)/shard_map/reduce_scatter | solution.py:161
  209.4 153.1 %all-to-all-start.2 = ((bf16[8,2,32,128]{3,2,1,0:T(8,128)(2,1)}), bf16[8,2,32,128]{3,2,1,0:T(8,128)(2,1)S(1)}, u32[]{:S(2)}, u32[]{:S(2)}) async-start(bf16[8,2,32,128]{3,2,1,0:T(8,128)(2,1)} %copy.27), calls=%async_computation.3 | async-start | bytes 262144 | tf_op jit(solution)/shard_map/all_to_all | solution.py:189
  212.8 219.4 %all-reduce.4.cloned.1.call-start = ((), (), s32[]{:S(2)}) async-start(), calls=%async_computation.7 | async-start | bytes 4718592 | tf_op jit(solution)/shard_map/psum | solution.py:181
  290.7 5.6 %copy-start.5 = (f32[32,768]{1,0:T(8,128)S(1)}, f32[32,768]{1,0:T(8,128)}, u32[]{:S(2)}) copy-start(f32[32,768]{1,0:T(8,128)} %reduce-scatter.3.cloned.1.call-done) | copy-start | bytes 294916
  362.5 28.0 %all-to-all-start.3 = ((bf16[4,2,32,128]{3,2,1,0:T(8,128)(2,1)}), bf16[4,2,32,128]{3,2,1,0:T(8,128)(2,1)S(1)}, u32[]{:S(2)}, u32[]{:S(2)}) async-start(bf16[4,2,32,128]{3,2,1,0:T(8,128)(2,1)} %copy.30), calls=%async_computation.4 | async-start | bytes 131072 | tf_op jit(solution)/shard_map/all_to_all | solution.py:205
  400.7 34.8 %copy-start.1 = (f32[768,768]{1,0:T(8,128)S(1)}, f32[768,768]{1,0:T(8,128)}, u32[]{:S(2)}) copy-start(f32[768,768]{1,0:T(8,128)} %param.10) | copy-start | bytes 7077892
Sparse Core Ops, SparseCore 0:
  205.7 17.4 reduce-scatter.4
  227.1 63.5 reduce-scatter.2
  296.8 135.3 all-reduce.3
where the time goes:
time: 445 us; the launch traced here: 443 us
  blocking collectives  206 us (46%)
  other arithmetic  78.7 us (18%)
  waiting for transfers between devices  70.1 us (16%)
  matrix products  27 us (6%)
  local copies, waits for them, and re-layouts  25.3 us (6%)
  between operations  18.5 us (4%)
  starting transfers between devices  17.8 us (4%)
    unnamed x1, blocking collectives  64.1 us
    psum x1, blocking collectives, shards(): lax.psum((jnp.sum(jnp.log(own_rows)) + jnp.sum(jnp.log(own_cols)), positi...  40.7 us
    all_gather x1, blocking collectives, shards(): lax.all_gather(unit_nodes, 'dev', axis=0, tiled=True)  32.1 us
    all_gather x1, blocking collectives, shards(): lax.all_gather(rounded_grads, 'dev', axis=0, tiled=True)  31.2 us
    reduce_scatter x1, waiting for transfers between devices, shards(): lax.psum_scatter(node_part, 'dev', scatter_dimension=0, tiled=True)  29.5 us
    psum x1, waiting for transfers between devices, shards(): grad_weight = lax.psum(weight_term, ('grp', 'dev'))  28.1 us
    scatter-add x1, other arithmetic, shards(): grad_blocks = empty_blocks.at[col_block].add(local_spread)  25.5 us
    scatter-add x2, other arithmetic, land_blocks(): total.at[block_index].add(jnp.where(valid[:, None, None], incoming, 0.0))  22 us
  transfers between devices with their start and end apart: 7, of which 3 were waited for; matrix products, arithmetic and copies ran while one was open for 22% of the time, Pallas kernels for 0%

commit v1 on v0

--- a/solution.py
+++ b/solution.py
@@ -178,7 +178,7 @@
     ) / text_norm
     pre_grad = node_back * gelu_slope(before)
     weight_term = lax.dot_general(chosen, pre_grad, (((0,), (0,)), ((), ())), precision=PRECISE)
-    grad_weight = lax.psum(weight_term, ("grp", "dev"))
+    grad_weight = jnp.sum(lax.all_gather(weight_term, ("grp", "dev")), axis=0)
     row_grads = lax.dot_general(pre_grad, weight, (((1,), (1,)), ((), ())), precision=PRECISE)
     rounded_grads = row_grads.astype(jnp.bfloat16)
     empty_blocks = jnp.zeros((blocks_dev, block_rows, feat_width), jnp.float32)

time: 445 us -> 725 us (1.63)
  waiting for transfers between devices: 70.1 us -> 322 us
  other arithmetic: 78.7 us -> 104 us
    all_gather x0 -> x1, waiting for transfers between devices: none -> 252 us  [shards(): grad_weight = jnp.sum(lax.all_gather(weight_term, ('grp', 'dev')), axis=0)]
    psum x1 -> x0, waiting for transfers between devices: 28.1 us -> none  [shards(): grad_weight = lax.psum(weight_term, ('grp', 'dev'))]
    reduce_scatter x1, waiting for transfers between devices: 29.5 us -> 57.5 us  [shards(): lax.psum_scatter(node_part, 'dev', scatter_dimension=0, tiled=True)]
    reduce_sum x0 -> x1, other arithmetic: none -> 25.1 us  [shards(): grad_weight = jnp.sum(lax.all_gather(weight_term, ('grp', 'dev')), axis=0)]
  transfers between devices with their start and end apart: 7 -> 7, of which waited for: 3 -> 3; matrix products, arithmetic and copies ran while one was open for 22% -> 14% of each run, Pallas kernels for 0% -> 0%
where the time goes in v1:
time: 725 us; the launch traced here: 723 us
  waiting for transfers between devices  322 us (44%)
  blocking collectives  212 us (29%)
  other arithmetic  104 us (14%)
  matrix products  27.1 us (4%)
  local copies, waits for them, and re-layouts  22.1 us (3%)
  starting transfers between devices  18.6 us (3%)
  between operations  18.5 us (3%)
    all_gather x1, waiting for transfers between devices, shards(): grad_weight = jnp.sum(lax.all_gather(weight_term, ('grp', 'dev')), axis=0)  252 us
    unnamed x1, blocking collectives  64 us
    reduce_scatter x1, waiting for transfers between devices, shards(): lax.psum_scatter(node_part, 'dev', scatter_dimension=0, tiled=True)  57.5 us
    psum x1, blocking collectives, shards(): lax.psum((jnp.sum(jnp.log(own_rows)) + jnp.sum(jnp.log(own_cols)), positi...  43.3 us
    all_gather x1, blocking collectives, shards(): lax.all_gather(rounded_grads, 'dev', axis=0, tiled=True)  33.3 us
    all_gather x1, blocking collectives, shards(): lax.all_gather(unit_nodes, 'dev', axis=0, tiled=True)  32.1 us
    scatter-add x1, other arithmetic, shards(): grad_blocks = empty_blocks.at[col_block].add(local_spread)  25.3 us
    reduce_sum x1, other arithmetic, shards(): grad_weight = jnp.sum(lax.all_gather(weight_term, ('grp', 'dev')), axis=0)  25.1 us
  transfers between devices with their start and end apart: 7, of which 3 were waited for; matrix products, arithmetic and copies ran while one was open for 14% of the time, Pallas kernels for 0%

profile of v1, /device:TPU:0, one launch (start us, length us, event | category | flops | bytes accessed | tf_op | source)
XLA Modules:
  0.0 723.3 jit_solution(17102007510393398845)
XLA Ops:
  7.2 0.9 reshape.393
  8.3 0.2 reduce_window_sum.29
  8.5 0.1 select_reduce_fusion.1
  8.7 0.2 fusion.39
  8.9 1.5 convert_element_type.25
  10.7 1.8 gather_fusion.3
  12.5 2.8 select_select_fusion.1
  15.3 4.4 all-to-all-start.1
  19.7 0.8 constant_dynamic-slice_fusion.1
  20.6 0.2 reduce_window_sum.27
  20.8 0.2 select_reduce_fusion
  21.1 2.5 gather_fusion.2
  23.7 0.1 fusion.26
  23.9 4.0 select_select_fusion
  27.9 12.5 %all-to-all-done.1 = bf16[4,2,128,768]{3,2,1,0:T(8,128)(2,1)} async-done(((bf16[4,2,128,768]{3,2,1,0:T(8,128)(2,1)}), bf16[4,2,128,768]{3,2,1,0:T(8,128)(2,1)}, u32[]{:S(2)}, u32[]{:S(2)}) %all-to-all-start.1) | async-done | bytes 1572896 | tf_op jit(solution)/shard_map/all_to_all | solution.py:112
  40.4 6.6 all-to-all-start
  47.1 2.1 gather_fusion
  49.4 2.8 gather_fusion.1
  52.2 0.6 dynamic-slice
  53.4 0.2 dynamic-update-slice
  53.7 64.0 %all-reduce = s32[256]{0:T(256)S(1)} all-reduce(s32[256]{0:T(256)S(1)} %dynamic-update-slice), channel_id=1, replica_groups=mesh['grp'=4,'dev'=8] {'dev'}, use_global_device_ids=true, to_apply=%add | all-reduce | flops 256 | bytes 2048
  117.7 0.8 constant_dynamic-slice_fusion.2
  118.5 0.2 convert_reduce_fusion
  119.0 6.6 all_gather.22
  125.6 1.1 bitcast_select_fusion.2
  126.8 5.8 pad_maximum_fusion
  132.6 6.0 gather_fusion.4
  138.6 3.6 fusion.7
  142.2 1.5 multiply_reduce_fusion.3
  143.9 32.1 %all_gather.21 = f32[256,768]{1,0:T(8,128)S(1)} all-gather(f32[32,768]{1,0:T(8,128)S(1)} %broadcast_divide_fusion.1), channel_id=1, replica_groups=mesh['grp'=4,'dev'=8] {'dev'}, dimensions={0}, use_global_device_ids=true | all-gather | bytes 884736 | tf_op jit(solution)/shard_map/all_gather | solution.py:142
  176.0 2.0 fusion.15
  178.0 19.6 %psum.28 = f32[256]{0:T(256)S(1)} all-reduce(f32[256]{0:T(256)S(1)} %get-tuple-element.6), channel_id=1, replica_groups=mesh['grp'=4,'dev'=8] {'dev'}, use_global_device_ids=true, to_apply=%region_10.11 | all-reduce | flops 256 | bytes 2048 | tf_op jit(solution)/shard_map/psum | solution.py:150
  197.6 5.6 psum.29
  203.3 2.8 convolution_multiply_fusion
  206.2 2.4 convolution_multiply_fusion.1
  208.6 57.5 %reduce-scatter.3.cloned.1.call-done = f32[32,768]{1,0:T(8,128)} async-done(((f32[256,768]{1,0:T(8,128)}), f32[32,768]{1,0:T(8,128)}) %reduce-scatter.3.cloned.1.call-update) | async-done | bytes 98320 | tf_op jit(solution)/shard_map/reduce_scatter | solution.py:161
  266.1 1.1 multiply_reduce_fusion.1
  267.2 4.5 fusion.57
  271.7 0.2 convolution_convert_fusion
  271.9 0.7 copy.27
  272.6 3.7 all-to-all-start.2
  276.5 0.2 convolution_convert_fusion.1
  276.7 0.6 copy.30
  277.3 0.7 log_reduce_fusion
  278.0 0.7 log_reduce_fusion.1
  279.9 43.3 %all-reduce.1 = (f32[]{:T(128)}, f32[]{:T(128)}) all-reduce(f32[]{:T(128)S(6)} %add.308, f32[]{:T(128)} %get-tuple-element.4), channel_id=1, replica_groups=mesh['grp'=4,'dev'=8] {'grp','dev'}, use_global_device_ids=true, to_apply=%region_15.16 | all-reduce | flops 2 | bytes 16 | tf_op jit(solution)/shard_map/psum | solution.py:169
  324.6 1.1 multiply_reduce_fusion
  325.7 1.6 subtract_divide_fusion
  327.3 2.3 fusion.63
  329.6 6.1 fusion.12
  335.7 1.3 broadcast_in_dim.214
  336.9 25.3 %scatter_fusion = f32[4,128,768]{2,1,0:T(8,128)} fusion(f32[4,128,768]{2,1,0:T(8,128)} %broadcast_in_dim.214, s32[28]{0:T(128)S(1)} %get-tuple-element.15, f32[28,128,768]{2,1,0:T(8,128)} %fusion.12), kind=kCustom, calls=%fused_computation.5 | custom fusion | flops 2752512 | bytes 33030256 | tf_op jit(solution)/shard_map/scatter-add | solution.py:188
  362.3 33.3 %all_gather.24 = bf16[256,768]{1,0:T(8,128)(2,1)S(1)} all-gather(bf16[32,768]{1,0:T(8,128)(2,1)S(1)} %get-tuple-element.34), channel_id=1, replica_groups=mesh['grp'=4,'dev'=8] {'dev'}, dimensions={0}, use_global_device_ids=true | all-gather | bytes 442368 | tf_op jit(solution)/shard_map/all_gather | solution.py:196
  395.6 3.7 all-to-all-start.3
  399.3 1.0 fusion.64
  400.4 3.5 bitcast_select_fusion
  403.8 14.6 %scatter_fusion.1 = f32[4,128,768]{2,1,0:T(8,128)} fusion(f32[4,128,768]{2,1,0:T(8,128)} %scatter_fusion, s32[16]{0:T(128)S(1)} %fusion.47, f32[16,128,768]{2,1,0:T(8,128)} %bitcast_select_fusion), kind=kCustom, calls=%fused_computation.6 | custom fusion | flops 1572864 | bytes 18874432 | tf_op jit(solution)/shard_map/scatter-add | solution.py:45
  418.4 7.1 all_gather.25
  425.5 0.6 fusion.65
  426.2 2.0 bitcast_select_fusion.1
  428.2 7.4 %scatter_fusion.2 = f32[4,128,768]{2,1,0:T(8,128)} fusion(f32[4,128,768]{2,1,0:T(8,128)} %scatter_fusion.1, s32[8]{0:T(128)S(1)} %fusion.48, f32[8,128,768]{2,1,0:T(8,128)} %bitcast_select_fusion.1), kind=kCustom, calls=%fused_computation.7 | custom fusion | flops 786432 | bytes 9437216 | tf_op jit(solution)/shard_map/scatter-add | solution.py:45
  435.6 3.4 scatter_fusion.3
  439.1 251.5 %all-gather.3.cloned.1.call-done = f32[24576,768]{1,0:T(8,128)} async-done(((f32[768,768]{1,0:T(8,128)}), f32[24576,768]{1,0:T(8,128)}) %all-gather.3.cloned.1.call-update) | async-done | bytes 75497488 | tf_op jit(solution)/shard_map/all_gather | solution.py:181
  690.6 25.1 %reduce_sum.131 = f32[768,768]{1,0:T(8,128)} reduce(f32[32,768,768]{2,1,0:T(8,128)} %bitcast.36, f32[]{:T(128)} %constant.203.clone.1), dimensions={0}, to_apply=%region_24.25 | reduce | flops 18284544 | bytes 77856768 | tf_op jit(solution)/shard_map/reduce_sum | solution.py:181
  (76 shorter events, 2.2 us)
Async XLA Ops:
  7.2 135.0 %copy-start = (f32[768,768]{1,0:T(8,128)S(1)}, f32[768,768]{1,0:T(8,128)}, u32[]{:S(2)}) copy-start(f32[768,768]{1,0:T(8,128)} %param.10) | copy-start | bytes 7077892
  15.3 25.1 %all-to-all-start.1 = ((bf16[4,2,128,768]{3,2,1,0:T(8,128)(2,1)}), bf16[4,2,128,768]{3,2,1,0:T(8,128)(2,1)}, u32[]{:S(2)}, u32[]{:S(2)}) async-start(bf16[4,2,128,768]{3,2,1,0:T(8,128)(2,1)} %select_select_fusion.1), calls=%async_computation.1 | async-start | bytes 3145728 | tf_op jit(solution)/shard_map/all_to_all | solution.py:112
  27.9 19.2 %copy-start.7 = (s32[32]{0:T(128)S(1)}, s32[32]{0:T(128)}, u32[]{:S(2)}) copy-start(s32[32]{0:T(128)} %param.12) | copy-start | bytes 388
  27.9 24.3 %copy-start.9 = (u32[32]{0:T(128)S(1)}, u32[32]{0:T(128)}, u32[]{:S(2)}) copy-start(u32[32]{0:T(128)} %constant.215) | copy-start | bytes 388
  27.9 25.5 %copy-start.8 = (s32[32]{0:T(128)S(1)}, s32[32]{0:T(128)}, u32[]{:S(2)}) copy-start(s32[32]{0:T(128)} %param.13) | copy-start | bytes 388
  27.9 90.8 %copy-start.3 = (f32[32,768]{1,0:T(8,128)S(1)}, f32[32,768]{1,0:T(8,128)}, u32[]{:S(2)}) copy-start(f32[32,768]{1,0:T(8,128)} %param.11) | copy-start | bytes 294916
  40.4 86.4 %all-to-all-start = ((bf16[8,2,128,768]{3,2,1,0:T(8,128)(2,1)}), bf16[8,2,128,768]{3,2,1,0:T(8,128)(2,1)}, u32[]{:S(2)}, u32[]{:S(2)}) async-start(bf16[8,2,128,768]{3,2,1,0:T(8,128)(2,1)} %select_select_fusion), calls=%async_computation | async-start | bytes 6291456 | tf_op jit(solution)/shard_map/all_to_all | solution.py:104
  47.1 219.0 %reduce-scatter.3.cloned.1.call-start = ((), (), s32[]{:S(2)}) async-start(), calls=%async_computation.6 | async-start | bytes 884736 | tf_op jit(solution)/shard_map/reduce_scatter | solution.py:161
  142.2 35.8 %copy-start.6 = (f32[32,768]{1,0:T(8,128)}, f32[32,768]{1,0:T(8,128)S(1)}, u32[]{:S(2)}) copy-start(f32[32,768]{1,0:T(8,128)S(1)} %fusion.7) | copy-start | bytes 294916
  142.2 33.8 %copy-start.2 = (f32[128,768]{1,0:T(8,128)S(1)}, f32[128,768]{1,0:T(8,128)}, u32[]{:S(2)}) copy-start(f32[128,768]{1,0:T(8,128)} %all_gather.22) | copy-start | bytes 1179652
  206.1 118.5 %reduce-scatter.5.cloned.1.call-start = ((), (), s32[]{:S(2)}) async-start(), calls=%async_computation.7 | async-start | bytes 491520 | tf_op jit(solution)/shard_map/reduce_scatter | solution.py:165
  208.5 482.1 %all-gather.3.cloned.1.call-start = ((), (), s32[]{:S(2)}) async-start(), calls=%async_computation.8 | async-start | bytes 77856768 | tf_op jit(solution)/shard_map/all_gather | solution.py:181
  267.2 57.4 %copy-start.4 = (f32[32,768]{1,0:T(8,128)S(1)}, f32[32,768]{1,0:T(8,128)}, u32[]{:S(2)}) copy-start(f32[32,768]{1,0:T(8,128)} %param.11) | copy-start | bytes 294916
  267.2 60.1 %copy-start.5 = (f32[32,768]{1,0:T(8,128)S(1)}, f32[32,768]{1,0:T(8,128)}, u32[]{:S(2)}) copy-start(f32[32,768]{1,0:T(8,128)} %reduce-scatter.3.cloned.1.call-done) | copy-start | bytes 294916
  272.6 123.0 %all-to-all-start.2 = ((bf16[8,2,32,128]{3,2,1,0:T(8,128)(2,1)}), bf16[8,2,32,128]{3,2,1,0:T(8,128)(2,1)S(1)}, u32[]{:S(2)}, u32[]{:S(2)}) async-start(bf16[8,2,32,128]{3,2,1,0:T(8,128)(2,1)} %copy.27), calls=%async_computation.3 | async-start | bytes 262144 | tf_op jit(solution)/shard_map/all_to_all | solution.py:189
  395.6 30.0 %all-to-all-start.3 = ((bf16[4,2,32,128]{3,2,1,0:T(8,128)(2,1)}), bf16[4,2,32,128]{3,2,1,0:T(8,128)(2,1)S(1)}, u32[]{:S(2)}, u32[]{:S(2)}) async-start(bf16[4,2,32,128]{3,2,1,0:T(8,128)(2,1)} %copy.30), calls=%async_computation.4 | async-start | bytes 131072 | tf_op jit(solution)/shard_map/all_to_all | solution.py:205
  690.6 25.1 %copy-start.1 = (f32[768,768]{1,0:T(8,128)S(1)}, f32[768,768]{1,0:T(8,128)}, u32[]{:S(2)}) copy-start(f32[768,768]{1,0:T(8,128)} %param.10) | copy-start | bytes 7077892
Sparse Core Ops, SparseCore 0:
  206.2 59.8 reduce-scatter.2
  268.6 20.0 reduce-scatter.4
  292.2 398.3 all-gather.2
